TPU v7x, 32 devices: a whole 2x2x4 slice. The times are simulated.
32 devices in a mesh: lon: 8 (over y, x, core), lat: 4 (over z).
Axes of the slice: x: 2, y: 2, z: 4, core: 2. Of those that a mesh axis runs over, the one named last changes fastest.
Arguments:
- normed: bfloat16 [8, 96, 192, 192], P(None, 'lat', 'lon'), may hold values from -6 to 6
- cotangent: bfloat16 [8, 96, 192, 192], P(None, 'lat', 'lon'), may hold values from -6 to 6
- weight_qkv: bfloat16 [192, 576], replicated, may hold values from -0.4375 to 0.4375
- weight_proj: bfloat16 [192, 192], replicated, may hold values from -0.4375 to 0.4375
- bias_table: bfloat16 [64, 6, 20736], P('lat'), may hold values from -6 to 390
Outputs:
- input_grad: bfloat16 [8, 96, 192, 192], P(None, 'lat', 'lon')
- qkv_grad: float32 [192, 576], replicated
- proj_grad: float32 [192, 192], replicated
- bias_grad: float32 [64, 6, 20736], P('lat')
All inputs are finite; a program needn't handle non-finite values.
Results may differ from a plain program's by a relative error of at most 0.019.
Values may be sent and summed in bfloat16 or wider, within the bound.
A program may use at most 192 MiB of HBM per device.

v0:
```python
import jax
import jax.numpy as jnp
from jax import lax
from jax.sharding import PartitionSpec as P

HEADS = 6
WIN_Z = 2
WIN_LAT = 6
WIN_LON = 12
WTOK = 144


def from_behind(block, axis, distance):
    devices = range(lax.axis_size(axis))
    route = [((i - distance) % len(devices), i) for i in devices]
    return lax.ppermute(block, axis, route)


def passed_along(block, axis, distance):
    devices = range(lax.axis_size(axis))
    route = [(i - distance, i) for i in devices if i - distance in devices]
    return lax.ppermute(block, axis, route)


def window_split(grid_field):
    levels, height, breadth = grid_field.shape[:3]
    trailing_dims = grid_field.shape[3:]
    shaped = grid_field.reshape(
        (levels // WIN_Z, WIN_Z, height // WIN_LAT, WIN_LAT, breadth // WIN_LON, WIN_LON)
        + trailing_dims
    )
    axes_order = (0, 2, 4, 1, 3, 5) + tuple(range(6, 6 + len(trailing_dims)))
    return shaped.transpose(axes_order).reshape((-1, WTOK) + trailing_dims)


def window_merge(windowed, levels, height, breadth):
    channels = windowed.shape[-1]
    shaped = windowed.reshape(
        levels // WIN_Z, height // WIN_LAT, breadth // WIN_LON, WIN_Z, WIN_LAT, WIN_LON, channels
    )
    return shaped.transpose(0, 3, 1, 4, 2, 5, 6).reshape(levels, height, breadth, channels)


def window_backward(
    block_in, block_cot, block_region, block_live, block_types, bias_rows, weight_qkv, weight_proj
):
    windows = block_in.shape[0]
    channels = block_in.shape[2]
    head_dim = channels // HEADS
    softmax_scale = head_dim ** (-0.5)
    high = lax.Precision.HIGHEST
    f32 = jnp.float32
    projected = jnp.einsum("bnc,cf->bnf", block_in, weight_qkv, preferred_element_type=f32).astype(
        jnp.bfloat16
    )
    projected = projected.reshape(windows, WTOK, 3, HEADS, head_dim)
    queries = projected[:, :, 0]
    key_rows = projected[:, :, 1]
    values = projected[:, :, 2]
    bias_add = jnp.dot(
        block_types.astype(jnp.bfloat16), bias_rows, preferred_element_type=f32
    ).reshape(windows, HEADS, WTOK, WTOK)
    scores = (
        jnp.einsum("bqhd,bkhd->bhqk", queries, key_rows, preferred_element_type=f32) * softmax_scale
        + bias_add
    )
    allowed = (block_region[:, :, None] == block_region[:, None, :]) & (
        block_live[:, :, None] == block_live[:, None, :]
    )
    allowed = allowed[:, None]
    peak_score = jnp.max(jnp.where(allowed, scores, -1e30), axis=-1, keepdims=True)
    exp_terms = jnp.where(allowed, jnp.exp(scores - peak_score), 0.0)
    attn_probs = exp_terms / jnp.sum(exp_terms, axis=-1, keepdims=True)
    probs_b = attn_probs.astype(jnp.bfloat16)
    mixed = jnp.einsum("bhqk,bkhd->bqhd", probs_b, values, preferred_element_type=f32).astype(
        jnp.bfloat16
    )
    mixed = mixed.reshape(windows, WTOK, channels)
    grad_proj = jnp.einsum("bnc,bnf->cf", mixed, block_cot, preferred_element_type=f32)
    mixed_grad = jnp.einsum(
        "bnf,cf->bnc", block_cot, weight_proj, preferred_element_type=f32
    ).astype(jnp.bfloat16)
    mixed_grad = mixed_grad.reshape(windows, WTOK, HEADS, head_dim)
    prob_grad = jnp.einsum("bqhd,bkhd->bhqk", mixed_grad, values, preferred_element_type=f32)
    row_delta = jnp.sum(attn_probs * prob_grad, axis=-1, keepdims=True)
    score_grad = attn_probs * (prob_grad - row_delta)
    grad_bias = jnp.dot(
        block_types.T, score_grad.reshape(windows, -1), precision=high, preferred_element_type=f32
    )
    score_grad_b = score_grad.astype(jnp.bfloat16)
    query_grad = (
        jnp.einsum("bhqk,bkhd->bqhd", score_grad_b, key_rows, preferred_element_type=f32)
        * softmax_scale
    ).astype(jnp.bfloat16)
    key_grad = (
        jnp.einsum("bhqk,bqhd->bkhd", score_grad_b, queries, preferred_element_type=f32)
        * softmax_scale
    ).astype(jnp.bfloat16)
    value_grad = jnp.einsum(
        "bhqk,bqhd->bkhd", probs_b, mixed_grad, preferred_element_type=f32
    ).astype(jnp.bfloat16)
    cols_grad = jnp.stack([query_grad, key_grad, value_grad], axis=2).reshape(
        windows, WTOK, 3 * channels
    )
    grad_qkv = jnp.einsum("bnc,bnf->cf", block_in, cols_grad, preferred_element_type=f32)
    grad_in = jnp.einsum("bnf,cf->bnc", cols_grad, weight_qkv, preferred_element_type=f32).astype(
        jnp.bfloat16
    )
    return (grad_in, grad_qkv, grad_proj, grad_bias)


def local(normed, cotangent, weight_qkv, weight_proj, bias_table):
    levels, height, breadth, channels = normed.shape
    level_shift = WIN_Z // 2
    lat_shift = WIN_LAT // 2
    lon_shift = WIN_LON // 2
    normed = jnp.roll(normed, -level_shift, axis=0)
    cotangent = jnp.roll(cotangent, -level_shift, axis=0)
    across = from_behind((normed[:, :, :lon_shift], cotangent[:, :, :lon_shift]), "lon", -1)
    wide_in = jnp.concatenate([normed[:, :, lon_shift:], across[0]], axis=2)
    wide_cot = jnp.concatenate([cotangent[:, :, lon_shift:], across[1]], axis=2)
    upward = passed_along((wide_in[:, :lat_shift], wide_cot[:, :lat_shift]), "lat", -1)
    frame_in = jnp.concatenate([wide_in[:, lat_shift:], upward[0]], axis=1)
    frame_cot = jnp.concatenate([wide_cot[:, lat_shift:], upward[1]], axis=1)
    is_last = lax.axis_index("lat") == lax.axis_size("lat") - 1
    row_index = jnp.arange(height, dtype=jnp.int32)
    live_rows = jnp.logical_not(is_last & (row_index >= height - lat_shift))
    live_field = jnp.broadcast_to(live_rows[None, :, None], (levels, height, breadth))
    level_index = jnp.arange(levels, dtype=jnp.int32)
    wrapped_levels = (level_index >= levels - level_shift).astype(jnp.int32)
    wrapped_field = jnp.broadcast_to(wrapped_levels[:, None, None], (levels, height, breadth))
    level_windows = levels // WIN_Z
    lat_windows = height // WIN_LAT
    lon_windows = breadth // WIN_LON
    types_local = level_windows * lat_windows
    level_part = jnp.arange(level_windows, dtype=jnp.int32)[:, None, None]
    lat_part = jnp.arange(lat_windows, dtype=jnp.int32)[None, :, None]
    kinds = jnp.broadcast_to(
        lat_part * level_windows + level_part, (level_windows, lat_windows, lon_windows)
    )
    onehot = (
        kinds.reshape(-1)[:, None] == jnp.arange(types_local, dtype=jnp.int32)[None, :]
    ).astype(jnp.float32)
    bias_rows = bias_table.reshape(types_local, -1)
    framed_in = window_split(frame_in)
    window_total = framed_in.shape[0]
    block_size = max((divisor for divisor in range(1, 17) if window_total % divisor == 0))
    blocks = window_total // block_size

    def regroup(array):
        return array.reshape((blocks, block_size) + array.shape[1:])

    def step_block(totals, pieces):
        grad_in, grad_qkv, grad_proj, grad_bias = window_backward(
            pieces[0],
            pieces[1],
            pieces[2],
            pieces[3],
            pieces[4],
            bias_rows,
            weight_qkv,
            weight_proj,
        )
        return ((totals[0] + grad_qkv, totals[1] + grad_proj, totals[2] + grad_bias), grad_in)

    start = (
        jnp.zeros((channels, 3 * channels), jnp.float32),
        jnp.zeros((channels, channels), jnp.float32),
        jnp.zeros((types_local, HEADS * WTOK * WTOK), jnp.float32),
    )
    pieces = (
        regroup(framed_in),
        regroup(window_split(frame_cot)),
        regroup(window_split(wrapped_field)),
        regroup(window_split(live_field)),
        regroup(onehot),
    )
    totals, grads = lax.scan(step_block, start, pieces)
    framed_grad = window_merge(grads.reshape(window_total, WTOK, channels), levels, height, breadth)
    returned = passed_along(framed_grad[:, height - lat_shift :], "lat", 1)
    wide_grad = jnp.concatenate([returned, framed_grad[:, : height - lat_shift]], axis=1)
    sideways = from_behind(wide_grad[:, :, breadth - lon_shift :], "lon", 1)
    shifted_grad = jnp.concatenate([sideways, wide_grad[:, :, : breadth - lon_shift]], axis=2)
    input_grad = jnp.roll(shifted_grad, level_shift, axis=0)
    lat_qkv, lat_proj = (
        lax.psum(totals[0].astype(jnp.bfloat16), "lat").astype(jnp.float32),
        lax.psum(totals[1].astype(jnp.bfloat16), "lat").astype(jnp.float32),
    )
    bias_grad, qkv_grad, proj_grad = (
        lax.psum(totals[2].astype(jnp.bfloat16), "lon").astype(jnp.float32),
        lax.psum(lat_qkv.astype(jnp.bfloat16), "lon").astype(jnp.float32),
        lax.psum(lat_proj.astype(jnp.bfloat16), "lon").astype(jnp.float32),
    )
    return (input_grad, qkv_grad, proj_grad, bias_grad.reshape(types_local, HEADS, WTOK * WTOK))


def solution(mesh):
    in_specs = (
        P(None, "lat", "lon", None),
        P(None, "lat", "lon", None),
        P(),
        P(),
        P("lat", None, None),
    )
    out_specs = (P(None, "lat", "lon", None), P(), P(), P("lat", None, None))
    return jax.shard_map(local, mesh=mesh, in_specs=in_specs, out_specs=out_specs, check_vma=False)
```

profile of v0, /device:TPU:0, one launch (start us, length us, event | category | flops | bytes accessed | tf_op | source)
XLA Modules:
  0.0 629.4 jit_solution(3365991301374217343)
XLA Ops:
  10.1 3.4 collective-permute-start
  25.9 4.3 copy.139
  37.8 3.2 slice_maximum_fusion
  60.9 4.0 copy.127
  64.9 4.0 reshape.130
  68.9 396.9 %while.17 = (s32[]{:T(128)}, f32[192,576]{1,0:T(8,128)}, f32[192,192]{1,0:T(8,128)}, f32[16,124416]{1,0:T(8,128)}, bf16[2,16,144,192]{3,1,0,2:T(8,128)(2,1)}, /*...) while((s32[]{:T(128)}, f32[192,576]{1,0:T(8,128)}, ...), condition=%wide.region_4.5_spmd.clone, body=%wide.region_0.4_spmd.clone.sunk | while | flops 3127491072 | bytes 382142976 | solution.py:178
  72.4 15.1 %dot_general.59 = bf16[6,144,144,16]{2,1,0,3:T(8,128)(2,1)} reshape(bf16[124416,16]{0,1:T(8,128)(2,1)} %bitcast.192) | data formatting | bytes 7962624 | tf_op jit(solution)/shard_map/while/body/eval_jaxpr/dot_general | solution.py:60
  87.5 12.4 %fusion.128 = f32[16,6,144,144]{3,0,2,1:T(8,128)} fusion(bf16[6,144,144,16]{2,1,0,3:T(8,128)(2,1)} %dot_general.59, f32[2,16,16]{2,1,0:T(8,128)S(1)} %get-tuple-element.332, s32[]{:T(128)S(6)} %copy.169), kind=kOutput, calls=%fused_computation.8.clone.1 | convolution fusion | flops 63700992 | bytes 11948036 | tf_op jit(solution)/shard_map/while/body/eval_jaxpr/dot_general | solution.py:60
  99.8 17.0 %copy.157 = f32[16,6,144,144]{2,3,1,0:T(8,128)} copy(f32[16,6,144,144]{3,0,2,1:T(8,128)} %fusion.128) | data formatting | bytes 15925248 | tf_op jit(solution)/shard_map/while/body/eval_jaxpr/dot_general | solution.py:60
  119.2 5.1 copy.158
  124.3 13.1 %multiply_add_fusion.2 = f32[16,6,144,144]{2,3,1,0:T(8,128)} fusion(f32[16,6,144,144]{2,3,1,0:T(8,128)} %copy.157, bf16[16,144,3,6,32]{1,4,3,2,0:T(8,128)(2,1)} %bitcast.182), kind=kOutput, calls=%fused_computation.7.clone.1 | convolution fusion | flops 131383296 | bytes 25264128 | tf_op jit(solution)/shard_map/while/body/eval_jaxpr/bqhd,bkhd->bhqk/dot_general | solution.py:64
  138.5 15.3 %fusion.129 = (f32[16,6,144]{2,1,0:T(8,128)S(1)}, f32[16,6,144,144]{2,3,1,0:T(8,128)}) fusion(f32[16,6,144,144]{2,3,1,0:T(8,128)} %multiply_add_fusion.2, pred[16,144,144]{1,2,0:T(8,128)(4,1)S(1)} %compare_and_fusion.2), kind=kOutput, calls=%fused_computation.93.clone.1 | output fusion | flops 7962767 | bytes 16312320 | tf_op jit(solution)/shard_map/while/body/eval_jaxpr/sub | solution.py:72
  153.8 8.0 %fusion.130 = bf16[16,144,1,6,32]{1,4,3,0,2:T(8,128)(2,1)S(1)} fusion(bf16[16,144,6,32]{1,3,2,0:T(8,128)(2,1)} %bitcast.193, f32[16,6,144,144]{2,3,1,0:T(8,128)} %get-tuple-element.289, f32[16,6,144]{2,1,0:T(8,128)S(1)} %get-tuple-element.290), kind=kOutput, calls=%fused_computation.33.clone.1 | convolution fusion | flops 131825664 | bytes 9787392 | tf_op jit(solution)/shard_map/while/body/eval_jaxpr/bhqk,bqhd->bkhd/dot_general | solution.py:99
  163.4 9.7 %multiply_reduce_fusion.2 = (f32[16,6,144]{2,1,0:T(8,128)S(1)}, f32[16,6,144,144]{2,3,1,0:T(8,128)}) fusion(f32[16,6,144,144]{2,3,1,0:T(8,128)S(1)} %copy-done.1, f32[16,6,144]{2,1,0:T(8,128)S(1)} %get-tuple-element.290, bf16[16,144,6,32]{1,3,2,0:T(8,128)(2,1)} %bitcast.194, bf16[16,144,3,6,32]{1,4,3,2,0:T(8,128)(2,1)} %bitcast.183), kind=kOutput, calls=%fused_computation.3.clone.1 | convolution fusion | flops 133360128 | bytes 19181568 | tf_op jit(solution)/shard_map/while/body/eval_jaxpr/bqhd,bkhd->bhqk/dot_general | solution.py:84
  173.1 10.1 %subtract_multiply_fusion.2 = f32[16,6,144,144]{2,3,1,0:T(8,128)S(1)} fusion(f32[16,6,144,144]{2,3,1,0:T(8,128)} %get-tuple-element.291, f32[16,6,144]{2,1,0:T(8,128)S(1)} %get-tuple-element.292, f32[16,6,144,144]{2,3,1,0:T(8,128)} %get-tuple-element.289, f32[16,6,144]{2,1,0:T(8,128)S(1)} %get-tuple-element.290), kind=kLoop, calls=%fused_computation.2.clone.1 | loop fusion | flops 5971968 | bytes 23998464 | tf_op jit(solution)/shard_map/while/body/eval_jaxpr/mul | solution.py:86
  183.2 5.0 fusion.131
  192.4 2.8 copy.159
  195.2 4.5 fusion.133
  199.7 6.8 %fusion.134 = bf16[16,6,32,144]{3,2,1,0:T(8,128)(2,1)S(1)} fusion(bf16[16,144,3,6,32]{1,4,3,2,0:T(8,128)(2,1)} %bitcast.186, f32[16,6,144,144]{2,3,1,0:T(8,128)} %get-tuple-element.289, f32[16,6,144]{2,1,0:T(8,128)S(1)} %copy-done.8), kind=kOutput, calls=%fused_computation.27.clone.1 | convolution fusion | flops 131825664 | bytes 16668672 | tf_op jit(solution)/shard_map/while/body/eval_jaxpr/bhqk,bkhd->bqhd/dot_general | solution.py:75
  207.2 17.1 %copy.160 = f32[16,6,144,144]{3,2,1,0:T(8,128)} copy(f32[16,6,144,144]{2,3,1,0:T(8,128)} %copy-done) | data formatting | bytes 15925248 | tf_op jit(solution)/shard_map/while/body/eval_jaxpr/mul | solution.py:86
  224.3 23.2 %reshape.132 = f32[16,124416]{1,0:T(8,128)} reshape(f32[16,6,144,144]{3,2,1,0:T(8,128)} %copy.160) | data formatting | bytes 15925248 | tf_op jit(solution)/shard_map/while/body/eval_jaxpr/reshape | solution.py:88
  247.5 11.2 %convolution_add_fusion.2 = f32[16,124416]{1,0:T(8,128)} fusion(f32[16,124416]{1,0:T(8,128)} %reshape.132, f32[16,124416]{1,0:T(8,128)} %get-tuple-element.311, pred[]{:T(512)S(6)} %compare.3, f32[2,16,16]{2,1,0:T(8,128)S(1)} %get-tuple-element.332, s32[]{:T(128)S(6)} %copy.169), kind=kOutput, calls=%fused_computation.1.clone.1 | convolution fusion | flops 386187264 | bytes 23896068 | tf_op jit(solution)/shard_map/while/body/eval_jaxpr/dot_general | solution.py:87
  265.9 15.1 %dot_general.59 = bf16[6,144,144,16]{2,1,0,3:T(8,128)(2,1)} reshape(bf16[124416,16]{0,1:T(8,128)(2,1)} %bitcast.192) | data formatting | bytes 7962624 | tf_op jit(solution)/shard_map/while/body/eval_jaxpr/dot_general | solution.py:60
  281.0 12.4 %fusion.128 = f32[16,6,144,144]{3,0,2,1:T(8,128)} fusion(bf16[6,144,144,16]{2,1,0,3:T(8,128)(2,1)} %dot_general.59, f32[2,16,16]{2,1,0:T(8,128)S(1)} %get-tuple-element.332, s32[]{:T(128)S(6)} %copy.169), kind=kOutput, calls=%fused_computation.8.clone.1 | convolution fusion | flops 63700992 | bytes 11948036 | tf_op jit(solution)/shard_map/while/body/eval_jaxpr/dot_general | solution.py:60
  293.4 17.0 %copy.157 = f32[16,6,144,144]{2,3,1,0:T(8,128)} copy(f32[16,6,144,144]{3,0,2,1:T(8,128)} %fusion.128) | data formatting | bytes 15925248 | tf_op jit(solution)/shard_map/while/body/eval_jaxpr/dot_general | solution.py:60
  312.7 4.8 copy.158
  317.6 13.1 %multiply_add_fusion.2 = f32[16,6,144,144]{2,3,1,0:T(8,128)} fusion(f32[16,6,144,144]{2,3,1,0:T(8,128)} %copy.157, bf16[16,144,3,6,32]{1,4,3,2,0:T(8,128)(2,1)} %bitcast.182), kind=kOutput, calls=%fused_computation.7.clone.1 | convolution fusion | flops 131383296 | bytes 25264128 | tf_op jit(solution)/shard_map/while/body/eval_jaxpr/bqhd,bkhd->bhqk/dot_general | solution.py:64
  331.7 15.3 %fusion.129 = (f32[16,6,144]{2,1,0:T(8,128)S(1)}, f32[16,6,144,144]{2,3,1,0:T(8,128)}) fusion(f32[16,6,144,144]{2,3,1,0:T(8,128)} %multiply_add_fusion.2, pred[16,144,144]{1,2,0:T(8,128)(4,1)S(1)} %compare_and_fusion.2), kind=kOutput, calls=%fused_computation.93.clone.1 | output fusion | flops 7962767 | bytes 16312320 | tf_op jit(solution)/shard_map/while/body/eval_jaxpr/sub | solution.py:72
  347.1 8.0 %fusion.130 = bf16[16,144,1,6,32]{1,4,3,0,2:T(8,128)(2,1)S(1)} fusion(bf16[16,144,6,32]{1,3,2,0:T(8,128)(2,1)} %bitcast.193, f32[16,6,144,144]{2,3,1,0:T(8,128)} %get-tuple-element.289, f32[16,6,144]{2,1,0:T(8,128)S(1)} %get-tuple-element.290), kind=kOutput, calls=%fused_computation.33.clone.1 | convolution fusion | flops 131825664 | bytes 9787392 | tf_op jit(solution)/shard_map/while/body/eval_jaxpr/bhqk,bqhd->bkhd/dot_general | solution.py:99
  356.6 9.7 %multiply_reduce_fusion.2 = (f32[16,6,144]{2,1,0:T(8,128)S(1)}, f32[16,6,144,144]{2,3,1,0:T(8,128)}) fusion(f32[16,6,144,144]{2,3,1,0:T(8,128)S(1)} %copy-done.1, f32[16,6,144]{2,1,0:T(8,128)S(1)} %get-tuple-element.290, bf16[16,144,6,32]{1,3,2,0:T(8,128)(2,1)} %bitcast.194, bf16[16,144,3,6,32]{1,4,3,2,0:T(8,128)(2,1)} %bitcast.183), kind=kOutput, calls=%fused_computation.3.clone.1 | convolution fusion | flops 133360128 | bytes 19181568 | tf_op jit(solution)/shard_map/while/body/eval_jaxpr/bqhd,bkhd->bhqk/dot_general | solution.py:84
  366.3 10.1 %subtract_multiply_fusion.2 = f32[16,6,144,144]{2,3,1,0:T(8,128)S(1)} fusion(f32[16,6,144,144]{2,3,1,0:T(8,128)} %get-tuple-element.291, f32[16,6,144]{2,1,0:T(8,128)S(1)} %get-tuple-element.292, f32[16,6,144,144]{2,3,1,0:T(8,128)} %get-tuple-element.289, f32[16,6,144]{2,1,0:T(8,128)S(1)} %get-tuple-element.290), kind=kLoop, calls=%fused_computation.2.clone.1 | loop fusion | flops 5971968 | bytes 23998464 | tf_op jit(solution)/shard_map/while/body/eval_jaxpr/mul | solution.py:86
  376.5 5.0 fusion.131
  388.5 4.5 fusion.133
  393.1 6.8 %fusion.134 = bf16[16,6,32,144]{3,2,1,0:T(8,128)(2,1)S(1)} fusion(bf16[16,144,3,6,32]{1,4,3,2,0:T(8,128)(2,1)} %bitcast.186, f32[16,6,144,144]{2,3,1,0:T(8,128)} %get-tuple-element.289, f32[16,6,144]{2,1,0:T(8,128)S(1)} %copy-done.8), kind=kOutput, calls=%fused_computation.27.clone.1 | convolution fusion | flops 131825664 | bytes 16668672 | tf_op jit(solution)/shard_map/while/body/eval_jaxpr/bhqk,bkhd->bqhd/dot_general | solution.py:75
  400.5 17.1 %copy.160 = f32[16,6,144,144]{3,2,1,0:T(8,128)} copy(f32[16,6,144,144]{2,3,1,0:T(8,128)} %copy-done) | data formatting | bytes 15925248 | tf_op jit(solution)/shard_map/while/body/eval_jaxpr/mul | solution.py:86
  417.6 23.2 %reshape.132 = f32[16,124416]{1,0:T(8,128)} reshape(f32[16,6,144,144]{3,2,1,0:T(8,128)} %copy.160) | data formatting | bytes 15925248 | tf_op jit(solution)/shard_map/while/body/eval_jaxpr/reshape | solution.py:88
  440.8 13.3 %convolution_add_fusion.2 = f32[16,124416]{1,0:T(8,128)} fusion(f32[16,124416]{1,0:T(8,128)} %reshape.132, f32[16,124416]{1,0:T(8,128)} %get-tuple-element.311, pred[]{:T(512)S(6)} %compare.3, f32[2,16,16]{2,1,0:T(8,128)S(1)} %get-tuple-element.332, s32[]{:T(128)S(6)} %copy.169), kind=kOutput, calls=%fused_computation.1.clone.1 | convolution fusion | flops 386187264 | bytes 23896068 | tf_op jit(solution)/shard_map/while/body/eval_jaxpr/dot_general | solution.py:87
  469.2 5.5 convert_element_type.82
  474.8 9.0 %reshape.117 = bf16[16,6,20736]{2,1,0:T(8,128)(2,1)} reshape(bf16[16,124416]{1,0:T(8,128)(2,1)} %convert_element_type.82) | data formatting | bytes 7962624 | tf_op jit(solution)/shard_map/reshape | solution.py:194
  483.8 21.9 %all-reduce.7.cloned.1.call-done = (bf16[192,576]{1,0:T(8,128)(2,1)}, bf16[192,192]{1,0:T(8,128)(2,1)}) async-done(((bf16[192,576]{1,0:T(8,128)(2,1)}, bf16[192,192]{1,0:T(8,128)(2,1)}), (bf16[192,576]{1,0:T(8,128)(2,1)}, bf16[192,192]{1,0:T(8,128)(2,1)})) %all-reduce.7.cloned.1.call-update) | async-done | bytes 294928 | tf_op jit(solution)/shard_map/psum | solution.py:186
  505.7 4.9 reshape_reshape.19
  510.6 3.9 copy.115
  514.5 5.2 reshape.116
  519.7 3.6 collective-permute-start.4
  523.5 4.5 collective-permute-done.4
  528.2 19.4 %collective-permute-done.5 = bf16[8,24,6,192]{3,0,2,1:T(8,128)(2,1)S(1)} collective-permute-done((bf16[8,24,6,192]{3,0,2,1:T(8,128)(2,1)S(1)}, bf16[8,24,6,192]{3,0,2,1:T(8,128)(2,1)S(1)}, u32[]{:S(2)}, u32[]{:S(2)}) %collective-permute-start.5) | collective-permute-done | bytes 442400 | tf_op jit(solution)/shard_map/ppermute | solution.py:16
  550.8 61.7 %all-reduce.5.cloned.1.call-done = (bf16[16,6,20736]{2,1,0:T(8,128)(2,1)}, bf16[192,576]{1,0:T(8,128)(2,1)}, bf16[192,192]{1,0:T(8,128)(2,1)}) async-done(((bf16[16,6,20736]{2,1,0:T(8,128)(2,1)}, bf16[192,576]{1,0:T(8,128)(2,1)}, bf16[192,192]{1,0:T(8,128)(2,1)}), (bf16[16,6,20736]{2,1,0:T(8,128)(2,1)}, bf16[192,576]{1,0:T(8,128)(2,1)}, bf16[192,192]{1,0:T(8,128)(2,1)})) %all-reduce.5.cloned.1.call-update) | async-done | bytes 4276240 | tf_op jit(solution)/shard_map/psum | solution.py:190
  615.8 6.5 %copy.117 = f32[16,6,20736]{2,0,1:T(8,128)} copy(bf16[16,6,20736]{2,1,0:T(8,128)(2,1)} %get-tuple-element.197) | data formatting | bytes 11943936
  (176 shorter events, 88.5 us)
Async XLA Ops:
  7.2 498.5 %all-reduce.7.cloned.1.call-start = ((), (), s32[]{:S(2)}) async-start(), calls=%async_computation.1 | async-start | bytes 688128 | tf_op jit(solution)/shard_map/psum | solution.py:186
  7.2 2.0 slice-start.3
  9.2 4.3 copy-start.9
  9.3 4.2 slice-start.4
  10.1 20.1 %collective-permute-start = (bf16[8,24,6,192]{3,1,2,0:T(8,128)(2,1)}, bf16[8,24,6,192]{3,1,2,0:T(8,128)(2,1)}, u32[]{:S(2)}, u32[]{:S(2)}) collective-permute-start(bf16[8,24,6,192]{3,1,2,0:T(8,128)(2,1)} %slice.92), channel_id=1, source_target_pairs={{4,0},{8,4},{12,8},{16,12},{20,16},{24,20},{28,24},{0,28},{5,1},{9... | collective-permute-start | bytes 1327112 | tf_op jit(solution)/shard_map/ppermute | solution.py:16
  16.8 15.9 %collective-permute-start.2 = (bf16[8,24,6,192]{3,1,2,0:T(8,128)(2,1)}, bf16[8,24,6,192]{3,1,2,0:T(8,128)(2,1)}, u32[]{:S(2)}, u32[]{:S(2)}) collective-permute-start(bf16[8,24,6,192]{3,1,2,0:T(8,128)(2,1)} %slice.96), channel_id=1, source_target_pairs={{4,0},{8,4},{12,8},{16,12},{20,16},{24,20},{28,24},{0,28},{5,1},{9... | collective-permute-start | bytes 1327112 | tf_op jit(solution)/shard_map/ppermute | solution.py:16
  18.0 2.2 copy-start.11
  25.9 4.3 copy-start.20
  31.4 11.8 %collective-permute-start.1 = (bf16[8,3,24,192]{3,2,1,0:T(8,128)(2,1)S(1)}, bf16[8,3,24,192]{3,2,1,0:T(8,128)(2,1)S(1)}, u32[]{:S(2)}, u32[]{:S(2)}) collective-permute-start(bf16[8,3,24,192]{3,2,1,0:T(8,128)(2,1)S(1)} %copy.101), channel_id=1, source_target_pairs={{1,0},{2,1},{3,2},{5,4},{6,5},{7,6},{9,8},{10,9},{11,10},{13,12},{... | collective-permute-start | bytes 663560 | tf_op jit(solution)/shard_map/ppermute | solution.py:22
  34.5 18.7 %collective-permute-start.3 = (bf16[8,3,24,192]{3,2,1,0:T(8,128)(2,1)}, bf16[8,3,24,192]{3,2,1,0:T(8,128)(2,1)}, u32[]{:S(2)}, u32[]{:S(2)}) collective-permute-start(bf16[8,3,24,192]{3,2,1,0:T(8,128)(2,1)} %copy.108), channel_id=1, source_target_pairs={{1,0},{2,1},{3,2},{5,4},{6,5},{7,6},{9,8},{10,9},{11,10},{13,12},{... | collective-permute-start | bytes 663560 | tf_op jit(solution)/shard_map/ppermute | solution.py:22
  69.2 18.3 %copy-start.3 = (bf16[2,16,144,192]{3,2,1,0:T(8,128)(2,1)}, bf16[2,16,144,192]{3,2,1,0:T(8,128)(2,1)S(1)}, u32[]{:S(2)}) copy-start(bf16[2,16,144,192]{3,2,1,0:T(8,128)(2,1)S(1)} %get-tuple-element.334) | copy-start | bytes 5308420 | tf_op jit(solution)/shard_map/while
  99.8 17.0 %copy-start.5 = (bf16[192,576]{1,0:T(8,128)(2,1)S(1)}, bf16[192,576]{1,0:T(8,128)(2,1)}, u32[]{:S(2)}) copy-start(bf16[192,576]{1,0:T(8,128)(2,1)} %get-tuple-element.329) | copy-start | bytes 663556 | tf_op jit(solution)/shard_map/while
  124.3 13.2 %copy-start.16 = (s32[2,16,144]{2,1,0:T(8,128)S(1)}, s32[2,16,144]{2,1,0:T(8,128)}, u32[]{:S(2)}) copy-start(s32[2,16,144]{2,1,0:T(8,128)} %get-tuple-element.330) | copy-start | bytes 55300 | tf_op jit(solution)/shard_map/while
  124.3 13.1 %copy-start.19 = (pred[2,16,144]{2,1,0:T(8,128)(4,1)S(1)}, pred[2,16,144]{2,1,0:T(8,128)(4,1)}, u32[]{:S(2)}) copy-start(pred[2,16,144]{2,1,0:T(8,128)(4,1)} %get-tuple-element.331) | copy-start | bytes 13828 | tf_op jit(solution)/shard_map/while
  153.8 19.3 %copy-start.7 = (f32[16,6,144]{2,1,0:T(8,128)}, f32[16,6,144]{2,1,0:T(8,128)S(1)}, u32[]{:S(2)}) copy-start(f32[16,6,144]{2,1,0:T(8,128)S(1)} %get-tuple-element.290) | copy-start | bytes 165892 | tf_op jit(solution)/shard_map/while
  153.8 9.6 %copy-start.1 = (f32[16,6,144,144]{2,3,1,0:T(8,128)S(1)}, f32[16,6,144,144]{2,3,1,0:T(8,128)}, u32[]{:S(2)}) copy-start(f32[16,6,144,144]{2,3,1,0:T(8,128)} %get-tuple-element.289) | copy-start | bytes 23887876 | tf_op jit(solution)/shard_map/while
  183.2 5.3 copy-start
  192.3 2.8 copy-start.2
  192.4 2.8 copy-start.14
  195.2 4.5 copy-start.8
  199.7 6.8 %copy-start.15 = (f32[192,576]{1,0:T(8,128)}, f32[192,576]{1,0:T(8,128)S(1)}, u32[]{:S(2)}) copy-start(f32[192,576]{1,0:T(8,128)S(1)} %fusion.133) | copy-start | bytes 1327108 | tf_op jit(solution)/shard_map/while
  199.7 6.8 %copy-start.4 = (bf16[2,16,144,192]{3,2,1,0:T(8,128)(2,1)S(1)}, bf16[2,16,144,192]{3,2,1,0:T(8,128)(2,1)}, u32[]{:S(2)}) copy-start(bf16[2,16,144,192]{3,2,1,0:T(8,128)(2,1)} %copy-done.3) | copy-start | bytes 5308420 | tf_op jit(solution)/shard_map/while
  199.7 6.8 %copy-start.17 = (f32[192,192]{1,0:T(8,128)S(1)}, f32[192,192]{1,0:T(8,128)}, u32[]{:S(2)}) copy-start(f32[192,192]{1,0:T(8,128)} %get-tuple-element.310) | copy-start | bytes 442372 | tf_op jit(solution)/shard_map/while
  207.2 17.1 %copy-start.18 = (f32[192,192]{1,0:T(8,128)}, f32[192,192]{1,0:T(8,128)S(1)}, u32[]{:S(2)}) copy-start(f32[192,192]{1,0:T(8,128)S(1)} %fusion.135) | copy-start | bytes 442372 | tf_op jit(solution)/shard_map/while
  224.3 34.4 %slice-start = ((s8[4718592]{0:T(1024)(128)(4,1)}), s8[524288]{0:T(1024)(128)(4,1)S(1)}, s32[]{:S(2)}) async-start(s8[4718592]{0:T(1024)(128)(4,1)} %bitcast.188), calls=%async_computation.2 | async-start | bytes 1048576 | tf_op jit(solution)/shard_map/while
  247.5 11.2 %slice-start.1 = ((s8[4718592]{0:T(1024)(128)(4,1)}), s8[4194304]{0:T(1024)(128)(4,1)S(1)}, s32[]{:S(2)}) async-start(s8[4718592]{0:T(1024)(128)(4,1)} %bitcast.188), calls=%async_computation.3 | async-start | bytes 8388608 | tf_op jit(solution)/shard_map/while
  247.5 11.2 %copy-start.6 = (bf16[192,576]{1,0:T(8,128)(2,1)S(1)}, bf16[192,576]{1,0:T(8,128)(2,1)}, u32[]{:S(2)}) copy-start(bf16[192,576]{1,0:T(8,128)(2,1)} %get-tuple-element.329) | copy-start | bytes 663556 | tf_op jit(solution)/shard_map/while
  258.7 1.7 copy-start.12
  262.7 18.3 %copy-start.3 = (bf16[2,16,144,192]{3,2,1,0:T(8,128)(2,1)}, bf16[2,16,144,192]{3,2,1,0:T(8,128)(2,1)S(1)}, u32[]{:S(2)}) copy-start(bf16[2,16,144,192]{3,2,1,0:T(8,128)(2,1)S(1)} %get-tuple-element.334) | copy-start | bytes 5308420 | tf_op jit(solution)/shard_map/while
  293.4 17.0 %copy-start.5 = (bf16[192,576]{1,0:T(8,128)(2,1)S(1)}, bf16[192,576]{1,0:T(8,128)(2,1)}, u32[]{:S(2)}) copy-start(bf16[192,576]{1,0:T(8,128)(2,1)} %get-tuple-element.329) | copy-start | bytes 663556 | tf_op jit(solution)/shard_map/while
  317.6 13.1 %copy-start.16 = (s32[2,16,144]{2,1,0:T(8,128)S(1)}, s32[2,16,144]{2,1,0:T(8,128)}, u32[]{:S(2)}) copy-start(s32[2,16,144]{2,1,0:T(8,128)} %get-tuple-element.330) | copy-start | bytes 55300 | tf_op jit(solution)/shard_map/while
  317.6 13.1 %copy-start.19 = (pred[2,16,144]{2,1,0:T(8,128)(4,1)S(1)}, pred[2,16,144]{2,1,0:T(8,128)(4,1)}, u32[]{:S(2)}) copy-start(pred[2,16,144]{2,1,0:T(8,128)(4,1)} %get-tuple-element.331) | copy-start | bytes 13828 | tf_op jit(solution)/shard_map/while
  347.1 19.3 %copy-start.7 = (f32[16,6,144]{2,1,0:T(8,128)}, f32[16,6,144]{2,1,0:T(8,128)S(1)}, u32[]{:S(2)}) copy-start(f32[16,6,144]{2,1,0:T(8,128)S(1)} %get-tuple-element.290) | copy-start | bytes 165892 | tf_op jit(solution)/shard_map/while
  347.1 9.6 %copy-start.1 = (f32[16,6,144,144]{2,3,1,0:T(8,128)S(1)}, f32[16,6,144,144]{2,3,1,0:T(8,128)}, u32[]{:S(2)}) copy-start(f32[16,6,144,144]{2,3,1,0:T(8,128)} %get-tuple-element.289) | copy-start | bytes 23887876 | tf_op jit(solution)/shard_map/while
  376.5 5.3 copy-start
  385.7 2.8 copy-start.2
  385.7 2.8 copy-start.14
  388.5 4.5 copy-start.8
  393.0 6.8 %copy-start.15 = (f32[192,576]{1,0:T(8,128)}, f32[192,576]{1,0:T(8,128)S(1)}, u32[]{:S(2)}) copy-start(f32[192,576]{1,0:T(8,128)S(1)} %fusion.133) | copy-start | bytes 1327108 | tf_op jit(solution)/shard_map/while
  393.0 6.8 %copy-start.4 = (bf16[2,16,144,192]{3,2,1,0:T(8,128)(2,1)S(1)}, bf16[2,16,144,192]{3,2,1,0:T(8,128)(2,1)}, u32[]{:S(2)}) copy-start(bf16[2,16,144,192]{3,2,1,0:T(8,128)(2,1)} %copy-done.3) | copy-start | bytes 5308420 | tf_op jit(solution)/shard_map/while
  393.0 6.8 %copy-start.17 = (f32[192,192]{1,0:T(8,128)S(1)}, f32[192,192]{1,0:T(8,128)}, u32[]{:S(2)}) copy-start(f32[192,192]{1,0:T(8,128)} %get-tuple-element.310) | copy-start | bytes 442372 | tf_op jit(solution)/shard_map/while
  400.5 17.1 %copy-start.18 = (f32[192,192]{1,0:T(8,128)}, f32[192,192]{1,0:T(8,128)S(1)}, u32[]{:S(2)}) copy-start(f32[192,192]{1,0:T(8,128)S(1)} %fusion.135) | copy-start | bytes 442372 | tf_op jit(solution)/shard_map/while
  417.6 36.5 %slice-start = ((s8[4718592]{0:T(1024)(128)(4,1)}), s8[524288]{0:T(1024)(128)(4,1)S(1)}, s32[]{:S(2)}) async-start(s8[4718592]{0:T(1024)(128)(4,1)} %bitcast.188), calls=%async_computation.2 | async-start | bytes 1048576 | tf_op jit(solution)/shard_map/while
  440.8 13.3 %slice-start.1 = ((s8[4718592]{0:T(1024)(128)(4,1)}), s8[4194304]{0:T(1024)(128)(4,1)S(1)}, s32[]{:S(2)}) async-start(s8[4718592]{0:T(1024)(128)(4,1)} %bitcast.188), calls=%async_computation.3 | async-start | bytes 8388608 | tf_op jit(solution)/shard_map/while
  440.8 13.3 %copy-start.6 = (bf16[192,576]{1,0:T(8,128)(2,1)S(1)}, bf16[192,576]{1,0:T(8,128)(2,1)}, u32[]{:S(2)}) copy-start(bf16[192,576]{1,0:T(8,128)(2,1)} %get-tuple-element.329) | copy-start | bytes 663556 | tf_op jit(solution)/shard_map/while
  469.2 143.3 %all-reduce.5.cloned.1.call-start = ((), (), s32[]{:S(2)}) async-start(), calls=%async_computation | async-start | bytes 11304960 | tf_op jit(solution)/shard_map/psum | solution.py:190
  519.7 8.3 %collective-permute-start.4 = (bf16[8,3,24,192]{3,0,2,1:T(8,128)(2,1)S(1)}, bf16[8,3,24,192]{3,0,2,1:T(8,128)(2,1)S(1)}, u32[]{:S(2)}, u32[]{:S(2)}) collective-permute-start(bf16[8,3,24,192]{3,0,2,1:T(8,128)(2,1)S(1)} %slice.99), channel_id=1, source_target_pairs={{0,1},{1,2},{2,3},{4,5},{5,6},{6,7},{8,9},{9,10},{10,11},{12,13},{... | collective-permute-start | bytes 663560 | tf_op jit(solution)/shard_map/ppermute | solution.py:22
  528.1 19.4 %collective-permute-start.5 = (bf16[8,24,6,192]{3,0,2,1:T(8,128)(2,1)S(1)}, bf16[8,24,6,192]{3,0,2,1:T(8,128)(2,1)S(1)}, u32[]{:S(2)}, u32[]{:S(2)}) collective-permute-start(bf16[8,24,6,192]{3,0,2,1:T(8,128)(2,1)S(1)} %pad_maximum_fusion.7), channel_id=1, source_target_pairs={{28,0},{0,4},{4,8},{8,12},{12,16},{16,20},{20,24},{24,28},{29,1},{... | collective-permute-start | bytes 1327112 | tf_op jit(solution)/shard_map/ppermute | solution.py:16
  (6 other events, 8.4 us)
Sparse Core Ops, SparseCore 0:
  469.3 36.3 all-reduce.6
  510.0 102.4 all-reduce.4
where the time goes:
time: 635 us; the launch traced here: 629 us
  local copies, waits for them, and re-layouts  244 us (38%)
  matrix products  161 us (25%)
  waiting for transfers between devices  110 us (17%)
  other arithmetic  79.9 us (13%)
  between operations  14.5 us (2%)
  starting transfers between devices  11.1 us (2%)
  loops' own time  9.27 us (1%)
    dot_general x4, local copies, waits for them, and re-layouts, window_backward(): jnp.dot(block_types.astype(jnp.bfloat16), bias_rows, preferred_element_ty...  64.3 us
    psum x1, waiting for transfers between devices, local(): lax.psum(totals[2].astype(jnp.bfloat16), 'lon').astype(jnp.float32)  61.7 us
    reshape x2, local copies, waits for them, and re-layouts, window_backward(): score_grad.reshape(windows, -1)  46.5 us
    mul x2, local copies, waits for them, and re-layouts, window_backward(): score_grad = attn_probs * (prob_grad - row_delta)  34.2 us
    sub x2, other arithmetic, window_backward(): exp_terms = jnp.where(allowed, jnp.exp(scores - peak_score), 0.0)  30.7 us
    dot_general x2, matrix products, window_backward(): jnp.einsum('bqhd,bkhd->bhqk', queries, key_rows, preferred_element_type=f32)  26.3 us
    dot_general x2, matrix products, window_backward(): jnp.dot(block_types.astype(jnp.bfloat16), bias_rows, preferred_element_ty...  24.7 us
    dot_general x2, matrix products, window_backward(): jnp.dot(block_types.T, score_grad.reshape(windows, -1), precision=high, p...  24.4 us
  transfers between devices with their start and end apart: 8, of which 5 were waited for; matrix products, arithmetic and copies ran while one was open for 10% of the time, Pallas kernels for 0%

commit v1 on v0

--- a/solution.py
+++ b/solution.py
@@ -187,7 +187,7 @@
         lax.psum(totals[1].astype(jnp.bfloat16), "lat").astype(jnp.float32),
     )
     bias_grad, qkv_grad, proj_grad = (
-        lax.psum(totals[2].astype(jnp.bfloat16), "lon").astype(jnp.float32),
+        jnp.sum(lax.all_gather(totals[2].astype(jnp.bfloat16), "lon"), axis=0).astype(jnp.float32),
         lax.psum(lat_qkv.astype(jnp.bfloat16), "lon").astype(jnp.float32),
         lax.psum(lat_proj.astype(jnp.bfloat16), "lon").astype(jnp.float32),
     )

time: 635 us -> 750 us (1.18)
  waiting for transfers between devices: 110 us -> 218 us
  other arithmetic: 79.9 us -> 97.3 us
  local copies, waits for them, and re-layouts: 244 us -> 235 us
    all_gather x0 -> x1, waiting for transfers between devices: none -> 150 us  [local(): lax.all_gather(totals[2].astype(jnp.bfloat16), 'lon')]
    psum x1, waiting for transfers between devices: 61.7 us -> 26.3 us  [local(): lax.psum(lat_qkv.astype(jnp.bfloat16), 'lon').astype(jnp.float32)]
    ppermute x3, waiting for transfers between devices: 19.4 us -> 0.01 us  [from_behind(): return lax.ppermute(block, axis, route)]
    psum x1, waiting for transfers between devices: 21.9 us -> 36.5 us  [local(): lax.psum(totals[0].astype(jnp.bfloat16), 'lat').astype(jnp.float32)]
    reduce_sum x0 -> x1, other arithmetic: none -> 14 us  [local(): jnp.sum(lax.all_gather(totals[2].astype(jnp.bfloat16), 'lon'), axis=0)]
    reshape x1 -> x0, local copies, waits for them, and re-layouts: 9.01 us -> none  [local(): bias_grad.reshape(types_local, HEADS, WTOK * WTOK)]
    unnamed x16 -> x17, local copies, waits for them, and re-layouts: 24.1 us -> 19 us
  transfers between devices with their start and end apart: 8 -> 9, of which waited for: 5 -> 5; matrix products, arithmetic and copies ran while one was open for 10% -> 8% of each run, Pallas kernels for 0% -> 0%
where the time goes in v1:
time: 750 us; the launch traced here: 745 us
  local copies, waits for them, and re-layouts  235 us (31%)
  waiting for transfers between devices  218 us (29%)
  matrix products  161 us (21%)
  other arithmetic  97.3 us (13%)
  between operations  14.2 us (2%)
  starting transfers between devices  11.1 us (1%)
  loops' own time  8.51 us (1%)
    all_gather x1, waiting for transfers between devices, local(): lax.all_gather(totals[2].astype(jnp.bfloat16), 'lon')  150 us
    dot_general x4, local copies, waits for them, and re-layouts, window_backward(): jnp.dot(block_types.astype(jnp.bfloat16), bias_rows, preferred_element_ty...  64.3 us
    reshape x2, local copies, waits for them, and re-layouts, window_backward(): score_grad.reshape(windows, -1)  46.5 us
    psum x1, waiting for transfers between devices, local(): lax.psum(totals[0].astype(jnp.bfloat16), 'lat').astype(jnp.float32)  36.5 us
    mul x2, local copies, waits for them, and re-layouts, window_backward(): score_grad = attn_probs * (prob_grad - row_delta)  34.2 us
    sub x2, other arithmetic, window_backward(): exp_terms = jnp.where(allowed, jnp.exp(scores - peak_score), 0.0)  30.7 us
    psum x1, waiting for transfers between devices, local(): lax.psum(lat_qkv.astype(jnp.bfloat16), 'lon').astype(jnp.float32)  26.3 us
    dot_general x2, matrix products, window_backward(): jnp.einsum('bqhd,bkhd->bhqk', queries, key_rows, preferred_element_type=f32)  26.3 us
  transfers between devices with their start and end apart: 9, of which 5 were waited for; matrix products, arithmetic and copies ran while one was open for 8% of the time, Pallas kernels for 0%

profile of v1, /device:TPU:0, one launch (start us, length us, event | category | flops | bytes accessed | tf_op | source)
XLA Modules:
  0.0 744.8 jit_solution(4067239483443858113)
XLA Ops:
  10.1 3.4 collective-permute-start
  25.9 4.3 copy.141
  37.8 3.2 slice_maximum_fusion
  60.9 4.0 copy.127
  64.9 4.0 reshape.128
  69.0 396.1 %while.17 = (s32[]{:T(128)}, f32[192,576]{1,0:T(8,128)}, f32[192,192]{1,0:T(8,128)}, f32[16,124416]{1,0:T(8,128)}, bf16[2,16,144,192]{3,1,0,2:T(8,128)(2,1)}, /*...) while((s32[]{:T(128)}, f32[192,576]{1,0:T(8,128)}, ...), condition=%wide.region_4.5_spmd.clone, body=%wide.region_0.4_spmd.clone.sunk | while | flops 3127491072 | bytes 382142976 | solution.py:178
  72.4 15.1 %dot_general.59 = bf16[6,144,144,16]{2,1,0,3:T(8,128)(2,1)} reshape(bf16[124416,16]{0,1:T(8,128)(2,1)} %bitcast.197) | data formatting | bytes 7962624 | tf_op jit(solution)/shard_map/while/body/eval_jaxpr/dot_general | solution.py:60
  87.5 12.4 %fusion.128 = f32[16,6,144,144]{3,0,2,1:T(8,128)} fusion(bf16[6,144,144,16]{2,1,0,3:T(8,128)(2,1)} %dot_general.59, f32[2,16,16]{2,1,0:T(8,128)S(1)} %get-tuple-element.331, s32[]{:T(128)S(6)} %copy.173), kind=kOutput, calls=%fused_computation.8.clone.1 | convolution fusion | flops 63700992 | bytes 11948036 | tf_op jit(solution)/shard_map/while/body/eval_jaxpr/dot_general | solution.py:60
  99.9 17.0 %copy.161 = f32[16,6,144,144]{2,3,1,0:T(8,128)} copy(f32[16,6,144,144]{3,0,2,1:T(8,128)} %fusion.128) | data formatting | bytes 15925248 | tf_op jit(solution)/shard_map/while/body/eval_jaxpr/dot_general | solution.py:60
  119.3 5.1 copy.162
  124.4 13.1 %multiply_add_fusion.2 = f32[16,6,144,144]{2,3,1,0:T(8,128)} fusion(f32[16,6,144,144]{2,3,1,0:T(8,128)} %copy.161, bf16[16,144,3,6,32]{1,4,3,2,0:T(8,128)(2,1)} %bitcast.187), kind=kOutput, calls=%fused_computation.7.clone.1 | convolution fusion | flops 131383296 | bytes 25264128 | tf_op jit(solution)/shard_map/while/body/eval_jaxpr/bqhd,bkhd->bhqk/dot_general | solution.py:64
  138.5 15.3 %fusion.129 = (f32[16,6,144]{2,1,0:T(8,128)S(1)}, f32[16,6,144,144]{2,3,1,0:T(8,128)}) fusion(f32[16,6,144,144]{2,3,1,0:T(8,128)} %multiply_add_fusion.2, pred[16,144,144]{1,2,0:T(8,128)(4,1)S(1)} %compare_and_fusion.2), kind=kOutput, calls=%fused_computation.94.clone.1 | output fusion | flops 7962767 | bytes 16312320 | tf_op jit(solution)/shard_map/while/body/eval_jaxpr/sub | solution.py:72
  153.9 8.0 %fusion.130 = bf16[16,144,1,6,32]{1,4,3,0,2:T(8,128)(2,1)S(1)} fusion(bf16[16,144,6,32]{1,3,2,0:T(8,128)(2,1)} %bitcast.198, f32[16,6,144,144]{2,3,1,0:T(8,128)} %get-tuple-element.288, f32[16,6,144]{2,1,0:T(8,128)S(1)} %get-tuple-element.289), kind=kOutput, calls=%fused_computation.33.clone.1 | convolution fusion | flops 131825664 | bytes 9787392 | tf_op jit(solution)/shard_map/while/body/eval_jaxpr/bhqk,bqhd->bkhd/dot_general | solution.py:99
  163.4 9.7 %multiply_reduce_fusion.2 = (f32[16,6,144]{2,1,0:T(8,128)S(1)}, f32[16,6,144,144]{2,3,1,0:T(8,128)}) fusion(f32[16,6,144,144]{2,3,1,0:T(8,128)S(1)} %copy-done.1, f32[16,6,144]{2,1,0:T(8,128)S(1)} %get-tuple-element.289, bf16[16,144,6,32]{1,3,2,0:T(8,128)(2,1)} %bitcast.199, bf16[16,144,3,6,32]{1,4,3,2,0:T(8,128)(2,1)} %bitcast.188), kind=kOutput, calls=%fused_computation.3.clone.1 | convolution fusion | flops 133360128 | bytes 19181568 | tf_op jit(solution)/shard_map/while/body/eval_jaxpr/bqhd,bkhd->bhqk/dot_general | solution.py:84
  173.1 10.1 %subtract_multiply_fusion.2 = f32[16,6,144,144]{2,3,1,0:T(8,128)S(1)} fusion(f32[16,6,144,144]{2,3,1,0:T(8,128)} %get-tuple-element.290, f32[16,6,144]{2,1,0:T(8,128)S(1)} %get-tuple-element.291, f32[16,6,144,144]{2,3,1,0:T(8,128)} %get-tuple-element.288, f32[16,6,144]{2,1,0:T(8,128)S(1)} %get-tuple-element.289), kind=kLoop, calls=%fused_computation.2.clone.1 | loop fusion | flops 5971968 | bytes 23998464 | tf_op jit(solution)/shard_map/while/body/eval_jaxpr/mul | solution.py:86
  183.2 5.0 fusion.131
  192.4 2.8 copy.163
  195.2 4.5 fusion.133
  199.8 6.8 fusion.134
  207.2 17.1 %copy.164 = f32[16,6,144,144]{3,2,1,0:T(8,128)} copy(f32[16,6,144,144]{2,3,1,0:T(8,128)} %copy-done) | data formatting | bytes 15925248 | tf_op jit(solution)/shard_map/while/body/eval_jaxpr/mul | solution.py:86
  224.3 23.2 %reshape.130 = f32[16,124416]{1,0:T(8,128)} reshape(f32[16,6,144,144]{3,2,1,0:T(8,128)} %copy.164) | data formatting | bytes 15925248 | tf_op jit(solution)/shard_map/while/body/eval_jaxpr/reshape | solution.py:88
  247.6 11.2 %convolution_add_fusion.2 = f32[16,124416]{1,0:T(8,128)} fusion(f32[16,124416]{1,0:T(8,128)} %reshape.130, f32[16,124416]{1,0:T(8,128)} %get-tuple-element.310, pred[]{:T(512)S(6)} %compare.3, f32[2,16,16]{2,1,0:T(8,128)S(1)} %get-tuple-element.331, s32[]{:T(128)S(6)} %copy.173), kind=kOutput, calls=%fused_computation.1.clone.1 | convolution fusion | flops 386187264 | bytes 23896068 | tf_op jit(solution)/shard_map/while/body/eval_jaxpr/dot_general | solution.py:87
  265.9 15.1 %dot_general.59 = bf16[6,144,144,16]{2,1,0,3:T(8,128)(2,1)} reshape(bf16[124416,16]{0,1:T(8,128)(2,1)} %bitcast.197) | data formatting | bytes 7962624 | tf_op jit(solution)/shard_map/while/body/eval_jaxpr/dot_general | solution.py:60
  281.1 12.4 %fusion.128 = f32[16,6,144,144]{3,0,2,1:T(8,128)} fusion(bf16[6,144,144,16]{2,1,0,3:T(8,128)(2,1)} %dot_general.59, f32[2,16,16]{2,1,0:T(8,128)S(1)} %get-tuple-element.331, s32[]{:T(128)S(6)} %copy.173), kind=kOutput, calls=%fused_computation.8.clone.1 | convolution fusion | flops 63700992 | bytes 11948036 | tf_op jit(solution)/shard_map/while/body/eval_jaxpr/dot_general | solution.py:60
  293.4 17.0 %copy.161 = f32[16,6,144,144]{2,3,1,0:T(8,128)} copy(f32[16,6,144,144]{3,0,2,1:T(8,128)} %fusion.128) | data formatting | bytes 15925248 | tf_op jit(solution)/shard_map/while/body/eval_jaxpr/dot_general | solution.py:60
  312.8 4.8 copy.162
  317.7 13.1 %multiply_add_fusion.2 = f32[16,6,144,144]{2,3,1,0:T(8,128)} fusion(f32[16,6,144,144]{2,3,1,0:T(8,128)} %copy.161, bf16[16,144,3,6,32]{1,4,3,2,0:T(8,128)(2,1)} %bitcast.187), kind=kOutput, calls=%fused_computation.7.clone.1 | convolution fusion | flops 131383296 | bytes 25264128 | tf_op jit(solution)/shard_map/while/body/eval_jaxpr/bqhd,bkhd->bhqk/dot_general | solution.py:64
  331.8 15.3 %fusion.129 = (f32[16,6,144]{2,1,0:T(8,128)S(1)}, f32[16,6,144,144]{2,3,1,0:T(8,128)}) fusion(f32[16,6,144,144]{2,3,1,0:T(8,128)} %multiply_add_fusion.2, pred[16,144,144]{1,2,0:T(8,128)(4,1)S(1)} %compare_and_fusion.2), kind=kOutput, calls=%fused_computation.94.clone.1 | output fusion | flops 7962767 | bytes 16312320 | tf_op jit(solution)/shard_map/while/body/eval_jaxpr/sub | solution.py:72
  347.2 8.1 %fusion.130 = bf16[16,144,1,6,32]{1,4,3,0,2:T(8,128)(2,1)S(1)} fusion(bf16[16,144,6,32]{1,3,2,0:T(8,128)(2,1)} %bitcast.198, f32[16,6,144,144]{2,3,1,0:T(8,128)} %get-tuple-element.288, f32[16,6,144]{2,1,0:T(8,128)S(1)} %get-tuple-element.289), kind=kOutput, calls=%fused_computation.33.clone.1 | convolution fusion | flops 131825664 | bytes 9787392 | tf_op jit(solution)/shard_map/while/body/eval_jaxpr/bhqk,bqhd->bkhd/dot_general | solution.py:99
  356.7 9.7 %multiply_reduce_fusion.2 = (f32[16,6,144]{2,1,0:T(8,128)S(1)}, f32[16,6,144,144]{2,3,1,0:T(8,128)}) fusion(f32[16,6,144,144]{2,3,1,0:T(8,128)S(1)} %copy-done.1, f32[16,6,144]{2,1,0:T(8,128)S(1)} %get-tuple-element.289, bf16[16,144,6,32]{1,3,2,0:T(8,128)(2,1)} %bitcast.199, bf16[16,144,3,6,32]{1,4,3,2,0:T(8,128)(2,1)} %bitcast.188), kind=kOutput, calls=%fused_computation.3.clone.1 | convolution fusion | flops 133360128 | bytes 19181568 | tf_op jit(solution)/shard_map/while/body/eval_jaxpr/bqhd,bkhd->bhqk/dot_general | solution.py:84
  366.4 10.1 %subtract_multiply_fusion.2 = f32[16,6,144,144]{2,3,1,0:T(8,128)S(1)} fusion(f32[16,6,144,144]{2,3,1,0:T(8,128)} %get-tuple-element.290, f32[16,6,144]{2,1,0:T(8,128)S(1)} %get-tuple-element.291, f32[16,6,144,144]{2,3,1,0:T(8,128)} %get-tuple-element.288, f32[16,6,144]{2,1,0:T(8,128)S(1)} %get-tuple-element.289), kind=kLoop, calls=%fused_computation.2.clone.1 | loop fusion | flops 5971968 | bytes 23998464 | tf_op jit(solution)/shard_map/while/body/eval_jaxpr/mul | solution.py:86
  376.6 5.0 fusion.131
  388.6 4.5 fusion.133
  393.1 6.8 fusion.134
  400.6 17.1 %copy.164 = f32[16,6,144,144]{3,2,1,0:T(8,128)} copy(f32[16,6,144,144]{2,3,1,0:T(8,128)} %copy-done) | data formatting | bytes 15925248 | tf_op jit(solution)/shard_map/while/body/eval_jaxpr/mul | solution.py:86
  417.7 23.2 %reshape.130 = f32[16,124416]{1,0:T(8,128)} reshape(f32[16,6,144,144]{3,2,1,0:T(8,128)} %copy.164) | data formatting | bytes 15925248 | tf_op jit(solution)/shard_map/while/body/eval_jaxpr/reshape | solution.py:88
  440.9 13.3 %convolution_add_fusion.2 = f32[16,124416]{1,0:T(8,128)} fusion(f32[16,124416]{1,0:T(8,128)} %reshape.130, f32[16,124416]{1,0:T(8,128)} %get-tuple-element.310, pred[]{:T(512)S(6)} %compare.3, f32[2,16,16]{2,1,0:T(8,128)S(1)} %get-tuple-element.331, s32[]{:T(128)S(6)} %copy.173), kind=kOutput, calls=%fused_computation.1.clone.1 | convolution fusion | flops 386187264 | bytes 23896068 | tf_op jit(solution)/shard_map/while/body/eval_jaxpr/dot_general | solution.py:87
  468.5 36.5 %all-reduce.7.cloned.1.call-done = (bf16[192,576]{1,0:T(8,128)(2,1)}, bf16[192,192]{1,0:T(8,128)(2,1)}) async-done(((bf16[192,576]{1,0:T(8,128)(2,1)}, bf16[192,192]{1,0:T(8,128)(2,1)}), (bf16[192,576]{1,0:T(8,128)(2,1)}, bf16[192,192]{1,0:T(8,128)(2,1)})) %all-reduce.7.cloned.1.call-update) | async-done | bytes 294928 | tf_op jit(solution)/shard_map/psum | solution.py:186
  505.1 5.6 convert_element_type.90
  510.7 4.9 reshape_reshape.19
  515.6 3.9 copy.115
  519.5 5.0 reshape.114
  525.9 3.6 collective-permute-start.4
  531.3 2.9 collective-permute-done.4
  535.2 26.3 %all-reduce.5.cloned.1.call-done = (bf16[192,576]{1,0:T(8,128)(2,1)}, bf16[192,192]{1,0:T(8,128)(2,1)}) async-done(((bf16[192,576]{1,0:T(8,128)(2,1)}, bf16[192,192]{1,0:T(8,128)(2,1)}), (bf16[192,576]{1,0:T(8,128)(2,1)}, bf16[192,192]{1,0:T(8,128)(2,1)})) %all-reduce.5.cloned.1.call-update) | async-done | bytes 294928 | tf_op jit(solution)/shard_map/psum | solution.py:191
  568.1 149.5 %all-gather.3.cloned.1.call-done = bf16[128,124416]{1,0:T(8,128)(2,1)} async-done(((bf16[16,124416]{1,0:T(8,128)(2,1)}), bf16[128,124416]{1,0:T(8,128)(2,1)}) %all-gather.3.cloned.1.call-update) | async-done | bytes 31850512 | tf_op jit(solution)/shard_map/all_gather | solution.py:190
  717.6 14.0 %reduce_sum.30 = bf16[16,124416]{1,0:T(8,128)(2,1)} reduce(bf16[8,16,124416]{2,1,0:T(8,128)(2,1)} %bitcast.200, bf16[]{:T(256)} %constant.26.clone.1), dimensions={0}, to_apply=%region_9.10 | reduce | flops 13934592 | bytes 35831808 | tf_op jit(solution)/shard_map/reduce_sum | solution.py:190
  734.2 3.8 copy.150
  (182 shorter events, 95.0 us)
Async XLA Ops:
  7.2 497.9 %all-reduce.7.cloned.1.call-start = ((), (), s32[]{:S(2)}) async-start(), calls=%async_computation.2 | async-start | bytes 688128 | tf_op jit(solution)/shard_map/psum | solution.py:186
  7.2 2.0 slice-start.3
  9.2 4.2 copy-start.10
  9.3 4.2 slice-start.4
  10.1 20.2 %collective-permute-start = (bf16[8,24,6,192]{3,1,2,0:T(8,128)(2,1)}, bf16[8,24,6,192]{3,1,2,0:T(8,128)(2,1)}, u32[]{:S(2)}, u32[]{:S(2)}) collective-permute-start(bf16[8,24,6,192]{3,1,2,0:T(8,128)(2,1)} %slice.92), channel_id=1, source_target_pairs={{4,0},{8,4},{12,8},{16,12},{20,16},{24,20},{28,24},{0,28},{5,1},{9... | collective-permute-start | bytes 1327112 | tf_op jit(solution)/shard_map/ppermute | solution.py:16
  16.8 15.9 %collective-permute-start.2 = (bf16[8,24,6,192]{3,1,2,0:T(8,128)(2,1)}, bf16[8,24,6,192]{3,1,2,0:T(8,128)(2,1)}, u32[]{:S(2)}, u32[]{:S(2)}) collective-permute-start(bf16[8,24,6,192]{3,1,2,0:T(8,128)(2,1)} %slice.96), channel_id=1, source_target_pairs={{4,0},{8,4},{12,8},{16,12},{20,16},{24,20},{28,24},{0,28},{5,1},{9... | collective-permute-start | bytes 1327112 | tf_op jit(solution)/shard_map/ppermute | solution.py:16
  18.1 2.2 copy-start.12
  25.9 4.3 copy-start.21
  31.4 11.8 %collective-permute-start.1 = (bf16[8,3,24,192]{3,2,1,0:T(8,128)(2,1)S(1)}, bf16[8,3,24,192]{3,2,1,0:T(8,128)(2,1)S(1)}, u32[]{:S(2)}, u32[]{:S(2)}) collective-permute-start(bf16[8,3,24,192]{3,2,1,0:T(8,128)(2,1)S(1)} %copy.101), channel_id=1, source_target_pairs={{1,0},{2,1},{3,2},{5,4},{6,5},{7,6},{9,8},{10,9},{11,10},{13,12},{... | collective-permute-start | bytes 663560 | tf_op jit(solution)/shard_map/ppermute | solution.py:22
  34.6 18.7 %collective-permute-start.3 = (bf16[8,3,24,192]{3,2,1,0:T(8,128)(2,1)}, bf16[8,3,24,192]{3,2,1,0:T(8,128)(2,1)}, u32[]{:S(2)}, u32[]{:S(2)}) collective-permute-start(bf16[8,3,24,192]{3,2,1,0:T(8,128)(2,1)} %copy.108), channel_id=1, source_target_pairs={{1,0},{2,1},{3,2},{5,4},{6,5},{7,6},{9,8},{10,9},{11,10},{13,12},{... | collective-permute-start | bytes 663560 | tf_op jit(solution)/shard_map/ppermute | solution.py:22
  69.2 18.3 %copy-start.3 = (bf16[2,16,144,192]{3,2,1,0:T(8,128)(2,1)}, bf16[2,16,144,192]{3,2,1,0:T(8,128)(2,1)S(1)}, u32[]{:S(2)}) copy-start(bf16[2,16,144,192]{3,2,1,0:T(8,128)(2,1)S(1)} %get-tuple-element.333) | copy-start | bytes 5308420 | tf_op jit(solution)/shard_map/while
  99.9 17.0 %copy-start.5 = (bf16[192,576]{1,0:T(8,128)(2,1)S(1)}, bf16[192,576]{1,0:T(8,128)(2,1)}, u32[]{:S(2)}) copy-start(bf16[192,576]{1,0:T(8,128)(2,1)} %get-tuple-element.328) | copy-start | bytes 663556 | tf_op jit(solution)/shard_map/while
  124.4 13.1 %copy-start.17 = (s32[2,16,144]{2,1,0:T(8,128)S(1)}, s32[2,16,144]{2,1,0:T(8,128)}, u32[]{:S(2)}) copy-start(s32[2,16,144]{2,1,0:T(8,128)} %get-tuple-element.329) | copy-start | bytes 55300 | tf_op jit(solution)/shard_map/while
  124.4 13.1 %copy-start.20 = (pred[2,16,144]{2,1,0:T(8,128)(4,1)S(1)}, pred[2,16,144]{2,1,0:T(8,128)(4,1)}, u32[]{:S(2)}) copy-start(pred[2,16,144]{2,1,0:T(8,128)(4,1)} %get-tuple-element.330) | copy-start | bytes 13828 | tf_op jit(solution)/shard_map/while
  153.9 19.3 %copy-start.7 = (f32[16,6,144]{2,1,0:T(8,128)}, f32[16,6,144]{2,1,0:T(8,128)S(1)}, u32[]{:S(2)}) copy-start(f32[16,6,144]{2,1,0:T(8,128)S(1)} %get-tuple-element.289) | copy-start | bytes 165892 | tf_op jit(solution)/shard_map/while
  153.9 9.6 %copy-start.1 = (f32[16,6,144,144]{2,3,1,0:T(8,128)S(1)}, f32[16,6,144,144]{2,3,1,0:T(8,128)}, u32[]{:S(2)}) copy-start(f32[16,6,144,144]{2,3,1,0:T(8,128)} %get-tuple-element.288) | copy-start | bytes 23887876 | tf_op jit(solution)/shard_map/while
  183.2 5.3 copy-start
  192.4 2.8 copy-start.2
  192.4 2.8 copy-start.15
  195.2 4.5 copy-start.8
  199.8 6.8 copy-start.16
  199.8 6.8 copy-start.4
  199.8 6.8 copy-start.18
  207.2 17.1 %copy-start.19 = (f32[192,192]{1,0:T(8,128)}, f32[192,192]{1,0:T(8,128)S(1)}, u32[]{:S(2)}) copy-start(f32[192,192]{1,0:T(8,128)S(1)} %fusion.135) | copy-start | bytes 442372 | tf_op jit(solution)/shard_map/while
  224.3 34.4 %slice-start = ((s8[4718592]{0:T(1024)(128)(4,1)}), s8[524288]{0:T(1024)(128)(4,1)S(1)}, s32[]{:S(2)}) async-start(s8[4718592]{0:T(1024)(128)(4,1)} %bitcast.193), calls=%async_computation.3 | async-start | bytes 1048576 | tf_op jit(solution)/shard_map/while
  247.6 11.2 %slice-start.1 = ((s8[4718592]{0:T(1024)(128)(4,1)}), s8[4194304]{0:T(1024)(128)(4,1)S(1)}, s32[]{:S(2)}) async-start(s8[4718592]{0:T(1024)(128)(4,1)} %bitcast.193), calls=%async_computation.4 | async-start | bytes 8388608 | tf_op jit(solution)/shard_map/while
  247.6 11.2 %copy-start.6 = (bf16[192,576]{1,0:T(8,128)(2,1)S(1)}, bf16[192,576]{1,0:T(8,128)(2,1)}, u32[]{:S(2)}) copy-start(bf16[192,576]{1,0:T(8,128)(2,1)} %get-tuple-element.328) | copy-start | bytes 663556 | tf_op jit(solution)/shard_map/while
  262.7 18.3 %copy-start.3 = (bf16[2,16,144,192]{3,2,1,0:T(8,128)(2,1)}, bf16[2,16,144,192]{3,2,1,0:T(8,128)(2,1)S(1)}, u32[]{:S(2)}) copy-start(bf16[2,16,144,192]{3,2,1,0:T(8,128)(2,1)S(1)} %get-tuple-element.333) | copy-start | bytes 5308420 | tf_op jit(solution)/shard_map/while
  293.4 17.0 %copy-start.5 = (bf16[192,576]{1,0:T(8,128)(2,1)S(1)}, bf16[192,576]{1,0:T(8,128)(2,1)}, u32[]{:S(2)}) copy-start(bf16[192,576]{1,0:T(8,128)(2,1)} %get-tuple-element.328) | copy-start | bytes 663556 | tf_op jit(solution)/shard_map/while
  317.7 13.1 %copy-start.17 = (s32[2,16,144]{2,1,0:T(8,128)S(1)}, s32[2,16,144]{2,1,0:T(8,128)}, u32[]{:S(2)}) copy-start(s32[2,16,144]{2,1,0:T(8,128)} %get-tuple-element.329) | copy-start | bytes 55300 | tf_op jit(solution)/shard_map/while
  317.7 13.1 %copy-start.20 = (pred[2,16,144]{2,1,0:T(8,128)(4,1)S(1)}, pred[2,16,144]{2,1,0:T(8,128)(4,1)}, u32[]{:S(2)}) copy-start(pred[2,16,144]{2,1,0:T(8,128)(4,1)} %get-tuple-element.330) | copy-start | bytes 13828 | tf_op jit(solution)/shard_map/while
  347.2 19.3 %copy-start.7 = (f32[16,6,144]{2,1,0:T(8,128)}, f32[16,6,144]{2,1,0:T(8,128)S(1)}, u32[]{:S(2)}) copy-start(f32[16,6,144]{2,1,0:T(8,128)S(1)} %get-tuple-element.289) | copy-start | bytes 165892 | tf_op jit(solution)/shard_map/while
  347.2 9.6 %copy-start.1 = (f32[16,6,144,144]{2,3,1,0:T(8,128)S(1)}, f32[16,6,144,144]{2,3,1,0:T(8,128)}, u32[]{:S(2)}) copy-start(f32[16,6,144,144]{2,3,1,0:T(8,128)} %get-tuple-element.288) | copy-start | bytes 23887876 | tf_op jit(solution)/shard_map/while
  376.5 5.3 copy-start
  385.7 2.8 copy-start.2
  385.7 2.8 copy-start.15
  388.6 4.5 copy-start.8
  393.1 6.8 copy-start.16
  393.1 6.8 copy-start.4
  393.1 6.8 copy-start.18
  400.6 17.1 %copy-start.19 = (f32[192,192]{1,0:T(8,128)}, f32[192,192]{1,0:T(8,128)S(1)}, u32[]{:S(2)}) copy-start(f32[192,192]{1,0:T(8,128)S(1)} %fusion.135) | copy-start | bytes 442372 | tf_op jit(solution)/shard_map/while
  417.7 36.5 %slice-start = ((s8[4718592]{0:T(1024)(128)(4,1)}), s8[524288]{0:T(1024)(128)(4,1)S(1)}, s32[]{:S(2)}) async-start(s8[4718592]{0:T(1024)(128)(4,1)} %bitcast.193), calls=%async_computation.3 | async-start | bytes 1048576 | tf_op jit(solution)/shard_map/while
  440.9 13.3 %slice-start.1 = ((s8[4718592]{0:T(1024)(128)(4,1)}), s8[4194304]{0:T(1024)(128)(4,1)S(1)}, s32[]{:S(2)}) async-start(s8[4718592]{0:T(1024)(128)(4,1)} %bitcast.193), calls=%async_computation.4 | async-start | bytes 8388608 | tf_op jit(solution)/shard_map/while
  440.9 13.3 %copy-start.6 = (bf16[192,576]{1,0:T(8,128)(2,1)S(1)}, bf16[192,576]{1,0:T(8,128)(2,1)}, u32[]{:S(2)}) copy-start(bf16[192,576]{1,0:T(8,128)(2,1)} %get-tuple-element.328) | copy-start | bytes 663556 | tf_op jit(solution)/shard_map/while
  468.5 93.0 %all-reduce.5.cloned.1.call-start = ((), (), s32[]{:S(2)}) async-start(), calls=%async_computation.1 | async-start | bytes 688128 | tf_op jit(solution)/shard_map/psum | solution.py:191
  505.1 212.5 %all-gather.3.cloned.1.call-start = ((), (), s32[]{:S(2)}) async-start(), calls=%async_computation | async-start | bytes 35831808 | tf_op jit(solution)/shard_map/all_gather | solution.py:190
  525.9 8.3 %collective-permute-start.4 = (bf16[8,3,24,192]{3,0,2,1:T(8,128)(2,1)S(1)}, bf16[8,3,24,192]{3,0,2,1:T(8,128)(2,1)S(1)}, u32[]{:S(2)}, u32[]{:S(2)}) collective-permute-start(bf16[8,3,24,192]{3,0,2,1:T(8,128)(2,1)S(1)} %slice.99), channel_id=1, source_target_pairs={{0,1},{1,2},{2,3},{4,5},{5,6},{6,7},{8,9},{9,10},{10,11},{12,13},{... | collective-permute-start | bytes 663560 | tf_op jit(solution)/shard_map/ppermute | solution.py:22
  535.2 29.7 %collective-permute-start.5 = (bf16[8,24,6,192]{3,0,2,1:T(8,128)(2,1)}, bf16[8,24,6,192]{3,0,2,1:T(8,128)(2,1)S(1)}, u32[]{:S(2)}, u32[]{:S(2)}) collective-permute-start(bf16[8,24,6,192]{3,0,2,1:T(8,128)(2,1)} %pad_maximum_fusion.7), channel_id=1, source_target_pairs={{28,0},{0,4},{4,8},{8,12},{12,16},{16,20},{20,24},{24,28},{29,1},{... | collective-permute-start | bytes 1327112 | tf_op jit(solution)/shard_map/ppermute | solution.py:16
  (8 other events, 11.5 us)
Sparse Core Ops, SparseCore 0:
  468.6 36.4 all-reduce.6
  508.3 53.1 all-reduce.4
  563.4 154.1 all-gather.2
